TPU v7x, 512 devices: a whole 4x8x8 slice. The times are simulated.
512 devices in a mesh: row: 16 (over z, core), col: 32 (over y, x).
Axes of the slice: x: 4, y: 8, z: 8, core: 2. Of those that a mesh axis runs over, the one named last changes fastest.
Arguments:
- ainv: float32 [4, 2048, 2, 4096], P(None, 'row', None, 'col'), may hold values from -6 to 6
- lhat_first: float32 [4, 2048, 512], P(None, ('row', 'col')), may hold values from -0.078125 to 0.078125
- lhat_second: float32 [4, 2048, 512], P(None, ('row', 'col')), may hold values from -0.09375 to 0.09375
- second_on_first: float32 [512, 512], replicated, may hold values from -0.25 to 0.25
- dinv_first: float32 [512, 512], P(None, 'col'), may hold values from -6 to 6
- dinv_second: float32 [512, 512], P(None, 'col'), may hold values from -6 to 6
- anc_first: int32 [48], replicated, may hold values from 0 to 63, as said below
- anc_second: int32 [32], replicated, may hold values from 0 to 63, as said below
Outputs:
- cross_first: float32 [4, 2048, 512], P(None, 'row', 'col')
- diag_first: float32 [512, 512], P(None, 'col')
- cross_second: float32 [4, 2048, 512], P(None, 'row', 'col')
- link_second: float32 [512, 512], P(None, 'col')
- diag_second: float32 [512, 512], P(None, 'col')
Inputs may be any that keep to these rules, and one draw needn't show every extreme that they name: `anc_first`: 48 different tile numbers in increasing order. `anc_second`: 32 different tile numbers in increasing order, each also listed in anc_first.
All inputs are finite; a program needn't handle non-finite values.
Results may differ from a plain program's by a relative error of at most 0.000088.
Values sent between devices are 32-bit elements; how exact they have to be, the bound alone decides.
A program may use at most 64 MiB of HBM per device.

v0:
```python
import jax
import jax.numpy as jnp
from jax import lax
from jax.sharding import PartitionSpec as P


def sent_to_all(array, axis):
    devices = lax.axis_size(axis)
    return lax.all_to_all(
        jnp.broadcast_to(array[None], (devices, *array.shape)), axis, 0, 0, tiled=True
    )


def in_order(pieces, dim):
    shape = list(pieces.shape[1:])
    shape[dim] *= pieces.shape[0]
    return jnp.moveaxis(pieces, 0, dim).reshape(shape)


def gather_directly(array, axis, dim):
    pieces = sent_to_all(array, axis)
    return in_order(pieces, dim)


def picked(array, axis, root):
    return lax.dynamic_index_in_dim(lax.all_gather(array, axis), root, 0, keepdims=False)


def split_up(array, dim, devices):
    shape = array.shape
    pieces = array.reshape(*shape[:dim], devices, shape[dim] // devices, *shape[dim + 1 :])
    return jnp.moveaxis(pieces, dim, 0)


def summed_on_arrival(array, axis, dim):
    pieces = split_up(array, dim, lax.axis_size(axis))
    arrived = lax.all_to_all(pieces, axis, split_axis=0, concat_axis=0, tiled=True)
    return arrived.sum(axis=0)


def gathered_total(array, axis):
    return lax.all_gather(array, axis).sum(0)


def product(left, right):
    return jnp.dot(left, right, precision=lax.Precision.HIGHEST, preferred_element_type=jnp.float32)


def inner(left, right):
    return lax.dot_general(
        left,
        right,
        (((0,), (0,)), ((), ())),
        precision=lax.Precision.HIGHEST,
        preferred_element_type=jnp.float32,
    )


def body(
    ainv, lhat_first, lhat_second, second_on_first, dinv_first, dinv_second, anc_first, anc_second
):
    row_count = lax.axis_size("row")
    col_count = lax.axis_size("col")
    own_row = lax.axis_index("row")
    own_col = lax.axis_index("col")
    local_rows, tile_size, strip_count, _ = ainv.shape
    panel_width = lhat_first.shape[2]
    column_share = dinv_first.shape[1]
    col_ratio = col_count // row_count
    square = ainv.reshape(local_rows * tile_size, strip_count * tile_size)
    row_tiles = jnp.arange(local_rows, dtype=jnp.int32) * row_count + own_row

    def tile_keep(listing):
        listed = jnp.any(row_tiles[:, None] == listing[None, :], axis=1)
        return listed.astype(jnp.float32)

    def panels(lhat, keep):
        whole = gather_directly(lhat, "col", 1)
        masked = whole * keep[:, None, None]
        grouped = masked.reshape(strip_count, col_ratio, tile_size, panel_width)
        chosen = lax.dynamic_index_in_dim(grouped, own_col // row_count, 1, keepdims=False)
        owned = picked(chosen, "row", own_col % row_count)
        return (
            masked.reshape(local_rows * tile_size, panel_width),
            owned.reshape(strip_count * tile_size, panel_width),
        )

    def reduce_cols(partial_value):
        return summed_on_arrival(partial_value, "col", 1)

    keep_first = tile_keep(anc_first)
    keep_second = tile_keep(anc_second)
    flat_first = jnp.repeat(keep_first, tile_size)[:, None]
    flat_second = jnp.repeat(keep_second, tile_size)[:, None]
    rows_first, cols_first = panels(lhat_first, keep_first)
    rows_second, cols_second = panels(lhat_second, keep_second)
    first_part = product(square, cols_first)
    cross_first = -flat_first * reduce_cols(first_part)
    top_slice = lax.dynamic_slice_in_dim(second_on_first, own_col * column_share, column_share, 0)
    second_part = product(square, cols_second) + product(cross_first, top_slice)
    cross_second = -flat_second * reduce_cols(second_part)
    diag_first = dinv_first - gathered_total(inner(rows_first, cross_first), "row")
    cross_term = inner(cross_first, rows_second)
    own_term = inner(diag_first, second_on_first)
    diag_term = inner(rows_second, cross_second)
    summed_cross, summed_diag = (
        gathered_total(cross_term, "row"),
        gathered_total(diag_term, "row"),
    )
    link_rows = -(summed_cross + own_term)
    link_local = lax.all_to_all(link_rows, "col", split_axis=1, concat_axis=0, tiled=True)
    diag_second = dinv_second - (summed_diag + inner(second_on_first, link_local))
    shape_out = (local_rows, tile_size, column_share)
    return (
        cross_first.reshape(shape_out),
        diag_first,
        cross_second.reshape(shape_out),
        link_local,
        diag_second,
    )


def solution(mesh):
    return jax.shard_map(
        body,
        mesh=mesh,
        in_specs=(
            P(None, "row", None, "col"),
            P(None, ("row", "col"), None),
            P(None, ("row", "col"), None),
            P(),
            P(None, "col"),
            P(None, "col"),
            P(),
            P(),
        ),
        out_specs=(
            P(None, "row", "col"),
            P(None, "col"),
            P(None, "row", "col"),
            P(None, "col"),
            P(None, "col"),
        ),
        check_vma=False,
    )
```

profile of v0, /device:TPU:1, one launch (start us, length us, event | category | flops | bytes accessed | tf_op | source)
XLA Modules:
  0.0 331.2 jit_solution(2227749758047834255)
XLA Ops:
  7.2 2.0 broadcast_in_dim.4
  9.3 10.5 %all-to-all-start = ((f32[32,4,4,512]{3,2,1,0:T(4,128)}), f32[32,4,4,512]{3,2,1,0:T(4,128)S(1)}, u32[]{:S(2)}, u32[]{:S(2)}) async-start(f32[32,4,4,512]{3,2,1,0:T(4,128)} %broadcast_in_dim.4), calls=%async_computation | async-start | bytes 2097152 | tf_op jit(solution)/shard_map/all_to_all | solution.py:9
  19.8 0.8 compare_reduce_fusion.1
  20.8 25.1 %all-to-all-done = f32[32,4,4,512]{3,2,1,0:T(4,128)S(1)} async-done(((f32[32,4,4,512]{3,2,1,0:T(4,128)}), f32[32,4,4,512]{3,2,1,0:T(4,128)S(1)}, u32[]{:S(2)}, u32[]{:S(2)}) %all-to-all-start) | async-done | bytes 1048608 | tf_op jit(solution)/shard_map/all_to_all | solution.py:9
  46.0 0.4 reshape.105
  46.4 0.9 dynamic-slice_multiply_fusion.1
  47.4 1.3 broadcast_in_dim.5
  48.7 6.4 %all-to-all-start.2 = ((f32[32,4,4,512]{3,2,1,0:T(4,128)}), f32[32,4,4,512]{3,2,1,0:T(4,128)S(1)}, u32[]{:S(2)}, u32[]{:S(2)}) async-start(f32[32,4,4,512]{3,2,1,0:T(4,128)} %broadcast_in_dim.5), calls=%async_computation.2 | async-start | bytes 2097152 | tf_op jit(solution)/shard_map/all_to_all | solution.py:9
  55.3 0.5 copy-done.8
  56.0 24.5 %all-to-all-done.2 = f32[32,4,4,512]{3,2,1,0:T(4,128)S(1)} async-done(((f32[32,4,4,512]{3,2,1,0:T(4,128)}), f32[32,4,4,512]{3,2,1,0:T(4,128)S(1)}, u32[]{:S(2)}, u32[]{:S(2)}) %all-to-all-start.2) | async-done | bytes 1048608 | tf_op jit(solution)/shard_map/all_to_all | solution.py:9
  80.5 1.1 copy-done.2
  81.5 1.3 copy.27
  82.9 1.4 reshape.110
  84.3 2.0 dynamic-slice_multiply_fusion
  86.3 23.3 %all-gather.8.cloned.1.call-done = f32[32,1,128,512]{3,2,1,0:T(8,128)} async-done(((f32[2,1,128,512]{3,2,1,0:T(8,128)}), f32[32,1,128,512]{3,2,1,0:T(8,128)}) %all-gather.8.cloned.1.call-update) | async-done | bytes 8388624 | tf_op jit(solution)/shard_map/all_gather | solution.py:26
  109.6 59.5 %all-gather.10.cloned.1.call-done = f32[32,1,128,512]{3,2,1,0:T(8,128)} async-done(((f32[2,1,128,512]{3,2,1,0:T(8,128)}), f32[32,1,128,512]{3,2,1,0:T(8,128)}) %all-gather.10.cloned.1.call-update) | async-done | bytes 8388624 | tf_op jit(solution)/shard_map/all_gather | solution.py:26
  169.1 2.1 constant_dynamic-slice_fusion
  171.2 3.9 %fusion.10 = f32[512,512]{1,0:T(8,128)} fusion(f32[256,512]{1,0:T(8,128)S(1)} %bitcast.71, f32[64,8,2,128]{3,2,1,0:T(2,128)} %bitcast.74), kind=kOutput, calls=%fused_computation.16 | convolution fusion | flops 805306368 | bytes 2097152 | tf_op jit(solution)/shard_map/dot_general | solution.py:46
  175.1 9.4 %all-to-all-start.1 = ((f32[32,512,16]{1,2,0:T(8,128)}), f32[32,512,16]{1,2,0:T(8,128)}, u32[]{:S(2)}, u32[]{:S(2)}) async-start(f32[32,512,16]{1,2,0:T(8,128)} %bitcast.65), calls=%async_computation.1 | async-start | bytes 2097152 | tf_op jit(solution)/shard_map/all_to_all | solution.py:37
  184.7 1.6 reshape.113
  186.3 1.3 reshape.109
  187.6 3.0 convolution_bitcast_fusion
  190.6 20.6 %all-to-all-done.1 = f32[32,512,16]{1,2,0:T(8,128)} async-done(((f32[32,512,16]{1,2,0:T(8,128)}), f32[32,512,16]{1,2,0:T(8,128)}, u32[]{:S(2)}, u32[]{:S(2)}) %all-to-all-start.1) | async-done | bytes 1048608 | tf_op jit(solution)/shard_map/all_to_all | solution.py:37
  211.3 1.3 reduce_sum.49
  212.6 0.7 fusion.7
  213.3 20.3 %all-gather.3 = f32[256,512]{1,0:T(8,128)} all-gather(f32[16,512]{1,0:T(8,128)S(1)} %fusion.7), channel_id=5, replica_groups=mesh['row'=16,'col'=32] {'row'}, dimensions={0}, use_global_device_ids=true | all-gather | bytes 557056 | tf_op jit(solution)/shard_map/all_gather | solution.py:42
  233.6 1.1 reduce_sum.54
  234.7 2.0 fusion.3
  236.7 16.3 %all-gather.1 = f32[8192,16]{0,1:T(8,128)S(1)} all-gather(f32[512,16]{0,1:T(8,128)S(1)} %fusion.3), channel_id=3, replica_groups=mesh['row'=16,'col'=32] {'row'}, dimensions={0}, use_global_device_ids=true | all-gather | bytes 557056 | tf_op jit(solution)/shard_map/all_gather | solution.py:42
  253.0 0.3 copy.35
  253.4 0.6 fusion
  254.2 0.8 copy.46
  255.0 1.7 reshape.121
  256.7 5.5 %all-to-all-start.4 = ((f32[32,1,256]{2,1,0:T(1,128)}), f32[32,1,256]{2,1,0:T(1,128)S(1)}, u32[]{:S(2)}, u32[]{:S(2)}) async-start(f32[32,1,256]{2,1,0:T(1,128)} %reshape.121), calls=%async_computation.4 | async-start | bytes 65536 | tf_op jit(solution)/shard_map/all_to_all | solution.py:111
  262.2 2.0 convolution_add_fusion
  264.2 6.6 %all-to-all-done.4 = f32[32,1,256]{2,1,0:T(1,128)S(1)} async-done(((f32[32,1,256]{2,1,0:T(1,128)}), f32[32,1,256]{2,1,0:T(1,128)S(1)}, u32[]{:S(2)}, u32[]{:S(2)}) %all-to-all-start.4) | async-done | bytes 32800 | tf_op jit(solution)/shard_map/all_to_all | solution.py:111
  270.8 3.9 %all-to-all-start.3 = ((f32[32,512,16]{1,2,0:T(8,128)}), f32[32,512,16]{1,2,0:T(8,128)S(1)}, u32[]{:S(2)}, u32[]{:S(2)}) async-start(f32[32,512,16]{1,2,0:T(8,128)} %bitcast.64), calls=%async_computation.3 | async-start | bytes 2097152 | tf_op jit(solution)/shard_map/all_to_all | solution.py:37
  274.8 0.7 convert_negate_fusion
  275.6 0.6 copy.31
  276.2 0.5 broadcast.33
  276.7 0.7 reduce
  277.6 0.7 copy.33
  278.3 22.4 %all-to-all-done.3 = f32[32,512,16]{1,2,0:T(8,128)S(1)} async-done(((f32[32,512,16]{1,2,0:T(8,128)}), f32[32,512,16]{1,2,0:T(8,128)S(1)}, u32[]{:S(2)}, u32[]{:S(2)}) %all-to-all-start.3) | async-done | bytes 1048608 | tf_op jit(solution)/shard_map/all_to_all | solution.py:37
  300.8 0.8 fusion.5
  301.6 20.5 %all-gather.4 = f32[8192,16]{0,1:T(8,128)S(1)} all-gather(f32[512,16]{0,1:T(8,128)S(1)} %fusion.5), channel_id=6, replica_groups=mesh['row'=16,'col'=32] {'row'}, dimensions={0}, use_global_device_ids=true | all-gather | bytes 557056 | tf_op jit(solution)/shard_map/all_gather | solution.py:42
  322.0 0.3 copy.36
  322.5 0.6 copy.32
  323.1 1.2 fusion.2
  (44 shorter events, 1.7 us)
Async XLA Ops:
  7.2 246.2 %copy-start = (f32[512,512]{1,0:T(8,128)S(1)}, f32[512,512]{1,0:T(8,128)}, u32[]{:S(2)}) copy-start(f32[512,512]{1,0:T(8,128)} %param.11) | copy-start | bytes 3145732
  7.2 40.2 %copy-start.4 = (f32[4,4,512]{2,1,0:T(4,128)S(1)}, f32[4,4,512]{2,1,0:T(4,128)}, u32[]{:S(2)}) copy-start(f32[4,4,512]{2,1,0:T(4,128)} %param.10) | copy-start | bytes 98308
  7.2 47.9 %copy-start.7 = (s32[32]{0:T(128)S(1)}, s32[32]{0:T(128)}, u32[]{:S(2)}) copy-start(s32[32]{0:T(128)} %param.15) | copy-start | bytes 388
  9.3 36.7 %all-to-all-start = ((f32[32,4,4,512]{3,2,1,0:T(4,128)}), f32[32,4,4,512]{3,2,1,0:T(4,128)S(1)}, u32[]{:S(2)}, u32[]{:S(2)}) async-start(f32[32,4,4,512]{3,2,1,0:T(4,128)} %broadcast_in_dim.4), calls=%async_computation | async-start | bytes 2097152 | tf_op jit(solution)/shard_map/all_to_all | solution.py:9
  19.8 89.9 %all-gather.8.cloned.1.call-start = ((), (), s32[]{:S(2)}) async-start(), calls=%async_computation.5 | async-start | bytes 8912896 | tf_op jit(solution)/shard_map/all_gather | solution.py:26
  48.7 31.8 %all-to-all-start.2 = ((f32[32,4,4,512]{3,2,1,0:T(4,128)}), f32[32,4,4,512]{3,2,1,0:T(4,128)S(1)}, u32[]{:S(2)}, u32[]{:S(2)}) async-start(f32[32,4,4,512]{3,2,1,0:T(4,128)} %broadcast_in_dim.5), calls=%async_computation.2 | async-start | bytes 2097152 | tf_op jit(solution)/shard_map/all_to_all | solution.py:9
  55.1 114.0 %all-gather.10.cloned.1.call-start = ((), (), s32[]{:S(2)}) async-start(), calls=%async_computation.6 | async-start | bytes 8912896 | tf_op jit(solution)/shard_map/all_gather | solution.py:26
  55.3 0.5 copy-start.8
  80.5 1.1 copy-start.2
  82.9 101.7 %copy-start.1 = (f32[4,32,4,512]{3,2,1,0:T(4,128)}, f32[4,32,4,512]{3,2,1,0:T(4,128)S(1)}, u32[]{:S(2)}) copy-start(f32[4,32,4,512]{3,2,1,0:T(4,128)S(1)} %copy.27) | copy-start | bytes 3145732
  171.2 82.2 %copy-start.5 = (f32[512,16]{0,1:T(8,128)S(1)}, f32[512,16]{0,1:T(8,128)}, u32[]{:S(2)}) copy-start(f32[512,16]{0,1:T(8,128)} %param.12) | copy-start | bytes 98308
  175.1 36.2 %all-to-all-start.1 = ((f32[32,512,16]{1,2,0:T(8,128)}), f32[32,512,16]{1,2,0:T(8,128)}, u32[]{:S(2)}, u32[]{:S(2)}) async-start(f32[32,512,16]{1,2,0:T(8,128)} %bitcast.65), calls=%async_computation.1 | async-start | bytes 2097152 | tf_op jit(solution)/shard_map/all_to_all | solution.py:37
  213.3 109.8 %copy-start.6 = (f32[512,16]{0,1:T(8,128)S(1)}, f32[512,16]{0,1:T(8,128)}, u32[]{:S(2)}) copy-start(f32[512,16]{0,1:T(8,128)} %param.13) | copy-start | bytes 98308
  253.4 71.0 %copy-start.3 = (f32[512,16]{0,1:T(8,128)}, f32[512,16]{0,1:T(8,128)S(1)}, u32[]{:S(2)}) copy-start(f32[512,16]{0,1:T(8,128)S(1)} %sub.12) | copy-start | bytes 98308
  256.7 14.1 %all-to-all-start.4 = ((f32[32,1,256]{2,1,0:T(1,128)}), f32[32,1,256]{2,1,0:T(1,128)S(1)}, u32[]{:S(2)}, u32[]{:S(2)}) async-start(f32[32,1,256]{2,1,0:T(1,128)} %reshape.121), calls=%async_computation.4 | async-start | bytes 65536 | tf_op jit(solution)/shard_map/all_to_all | solution.py:111
  270.8 29.9 %all-to-all-start.3 = ((f32[32,512,16]{1,2,0:T(8,128)}), f32[32,512,16]{1,2,0:T(8,128)S(1)}, u32[]{:S(2)}, u32[]{:S(2)}) async-start(f32[32,512,16]{1,2,0:T(8,128)} %bitcast.64), calls=%async_computation.3 | async-start | bytes 2097152 | tf_op jit(solution)/shard_map/all_to_all | solution.py:37
Sparse Core Ops, SparseCore 0:
  47.5 62.0 all-gather.7
  111.7 57.2 all-gather.9
where the time goes:
time: 332 us; the launch traced here: 331 us
  waiting for transfers between devices  182 us (55%)
  blocking collectives  57.1 us (17%)
  starting transfers between devices  35.8 us (11%)
  local copies, waits for them, and re-layouts  19.5 us (6%)
  matrix products  14.3 us (4%)
  between operations  14.3 us (4%)
  other arithmetic  8.25 us (2%)
    all_gather x2, waiting for transfers between devices, picked(): lax.all_gather(array, axis)  82.8 us
    all_gather x3, blocking collectives, gathered_total(): return lax.all_gather(array, axis).sum(0)  57.1 us
    all_to_all x2, waiting for transfers between devices, sent_to_all(): lax.all_to_all(jnp.broadcast_to(array[None], (devices, *array.shape)), ax...  49.6 us
    all_to_all x2, waiting for transfers between devices, summed_on_arrival(): lax.all_to_all(pieces, axis, split_axis=0, concat_axis=0, tiled=True)  43.1 us
    all_to_all x2, starting transfers between devices, sent_to_all(): lax.all_to_all(jnp.broadcast_to(array[None], (devices, *array.shape)), ax...  16.9 us
    all_to_all x2, starting transfers between devices, summed_on_arrival(): lax.all_to_all(pieces, axis, split_axis=0, concat_axis=0, tiled=True)  13.3 us
    dot_general x3, matrix products, product(): jnp.dot(left, right, precision=lax.Precision.HIGHEST, preferred_element_t...  8.95 us
  transfers between devices with their start and end apart: 7, of which 7 were waited for; matrix products, arithmetic and copies ran while one was open for 6% of the time, Pallas kernels for 0%

commit v1 on v0

v1 whole, which is shorter than its diff:
```python
import functools

import jax
import jax.numpy as jnp
from jax import lax
from jax.experimental import pallas as pl
from jax.experimental.pallas import tpu as pltpu
from jax.sharding import PartitionSpec as P

MESH = pl.DeviceIdType.MESH
F32 = jnp.float32
BF16 = jnp.bfloat16
X, Y, Z = 4, 8, 8
NR, NC = 16, 32


def split(value):
    high = value.astype(BF16)
    return high, (value - high.astype(F32)).astype(BF16)


def mm(left, right):
    return jnp.dot(left, right, preferred_element_type=F32)


def mm3(left, right_high, right_low):
    high, low = split(left)
    return mm(high, right_high) + (mm(low, right_high) + mm(high, right_low))


def kernel(
    a_hbm, s_hbm, l1_ref, l2_ref, d1_ref, d2_ref, anc1_ref, anc2_ref,
    cross1_ref, diag1_ref, cross2_ref, link_ref, diag2_ref,
    abuf, sbuf, s_high, s_low, rbuf, own, mbuf, m_high, m_low, pt, cr,
    tt, ts, tr, ls, lr, r0, tg, tsum, gb, lsum, xt, lk,
    local_sem, a_send, a_recv, my_send, my_recv, mx_send, mx_recv, sc_send, sc_recv,
    ag_send, ag_recv, dd_send, dd_recv, rs_send, rs_recv, t_send, t_recv, l_send, l_recv,
    tg_send, tg_recv, g_send, g_recv, b_send, b_recv,
):
    r, c = lax.axis_index("row"), lax.axis_index("col")
    z, core = r // 2, r % 2
    y, x = c // X, c % X
    right, left = (x + 1) % X, (x + X - 1) % X
    across = (x + 2) % X

    def remote(src, dst, send, recv, row, col):
        return pltpu.make_async_remote_copy(
            src_ref=src, dst_ref=dst, send_sem=send, recv_sem=recv,
            device_id=(row, col), device_id_type=MESH,
        )

    sent = []

    def start(copy):
        copy.start()
        sent.append(copy)

    a_copy = pltpu.make_async_copy(a_hbm, abuf.at[x], local_sem.at[0])
    a_copy.start()
    s_copy = pltpu.make_async_copy(s_hbm, sbuf, local_sem.at[1])
    s_copy.start()

    tile_ids = lax.broadcasted_iota(jnp.int32, (4, 1), 0) * NR + r

    def keeps(anc_ref):
        hits = jnp.where(anc_ref[...] == tile_ids, 1.0, 0.0).astype(F32)
        return jnp.max(hits, axis=1, keepdims=True)

    keep1, keep2 = keeps(anc1_ref), keeps(anc2_ref)
    rows1 = [l1_ref[a] * keep1[a : a + 1] for a in range(4)]
    rows2 = [l2_ref[a] * keep2[a : a + 1] for a in range(4)]

    def a_part(slot, half):
        return abuf.at[slot, pl.ds(half * 512, 512)]

    def a_move(slot, half, send, to):
        part = a_part(slot, half)
        return remote(part, part, a_send.at[send], a_recv.at[slot, half], r, y * X + to)

    a_copy.wait()
    start(a_move(x, 0, 0, right))
    start(a_move(x, 1, 1, left))
    start(a_move(x, 1, 2, right))
    start(a_move(x, 0, 3, left))

    s_copy.wait()
    sh, sl = split(sbuf[...])
    s_high[...] = sh
    s_low[...] = sl
    m1 = jnp.concatenate(rows1, axis=0)
    n2 = jnp.concatenate(rows2, axis=0) - mm3(m1, s_high[...], s_low[...])
    for a in range(4):
        yh, s = a % 2, a // 2
        for k in range(4):
            lanes = slice(k * 128, (k + 1) * 128)
            own[yh, k, s, pl.ds(0, 4, stride=2), :] = rows1[a][:, lanes]
            own[yh, k, s, pl.ds(1, 4, stride=2), :] = n2[a * 4 : a * 4 + 4, lanes]
    xs = r % X
    for yh in range(2):
        for k in range(4):
            to_col = (r // X + 4 * yh) * X + k
            here = jnp.logical_and(c // 2 == r, c == to_col)
            copy = remote(
                own.at[yh, k], mbuf.at[xs, :, c], sc_send.at[yh, k], sc_recv.at[xs, c % 2],
                c // 2, to_col,
            )

            @pl.when(jnp.logical_not(here))
            def _():
                copy.start()

            @pl.when(here)
            def _():
                mbuf[xs, :, c] = own[yh, k]

    rflat = rbuf
    for a in range(4):
        for k in range(4):
            lanes = slice(k * 128, (k + 1) * 128)
            rflat[a, y, x, pl.ds(k, 4, stride=8), :] = rows1[a][:, lanes]
            rflat[a, y, x, pl.ds(4 + k, 4, stride=8), :] = rows2[a][:, lanes]

    for xq in range(4):
        for par in range(2):
            from_row = (y % 4) * X + xq
            from_col = 2 * r + par
            here = jnp.logical_and(from_row == r, from_col == c)
            copy = remote(
                own.at[0, 0], mbuf.at[xq, :, from_col], sc_send.at[0, 0], sc_recv.at[xq, par],
                from_row, from_col,
            )

            @pl.when(jnp.logical_not(here))
            def _():
                copy.wait_recv()

    def slab(row):
        return mbuf.at[:, :, pl.ds(2 * row, 2)]

    for d in (1, 7, 2, 6, 3, 5, 4):
        to = (z + d) % Z
        start(remote(slab(r), slab(r), ag_send.at[d], ag_recv.at[z], to * 2 + core, c))
    start(remote(slab(r), slab(r), dd_send.at[z], dd_recv.at[z], z * 2 + 1 - core, c))

    def r_part(yy, xx):
        return rbuf.at[:, yy, xx]

    for d in (1, 7, 2, 6, 3, 5, 4):
        to = (y + d) % Y
        start(remote(r_part(y, x), r_part(y, x), my_send.at[d], my_recv.at[y], r, to * X + x))

    def a_wait(slot, half):
        a_move(slot, half, 0, right).wait_recv()

    a_wait(left, 0)
    start(a_move(left, 0, 4, right))
    a_wait(right, 1)
    start(a_move(right, 1, 5, left))

    for d in (7, 1, 6, 2, 5, 3, 4):
        zs = (z + d) % Z
        part = slab(zs * 2 + core)
        remote(part, part, ag_send.at[d], ag_recv.at[zs], r, c).wait_recv()
        start(remote(part, part, dd_send.at[zs], dd_recv.at[zs], z * 2 + 1 - core, c))

    d1 = d1_ref[...]
    r0_full = mm3(d1, s_high[...], s_low[...])
    for k in range(4):
        r0[k] = r0_full[:, k * 128 : (k + 1) * 128]

    for d in (7, 1, 6, 2, 5, 3, 4):
        ys = (y + d) % Y
        part = r_part(ys, x)
        remote(part, part, my_send.at[d], my_recv.at[ys], r, c).wait_recv()

    def r_move(slot, half, send, to):
        part = rbuf.at[pl.ds(half * 2, 2), :, slot]
        return remote(part, part, mx_send.at[send], mx_recv.at[slot, half], r, y * X + to)

    start(r_move(x, 0, 0, right))
    start(r_move(x, 1, 1, left))
    start(r_move(x, 1, 2, right))
    start(r_move(x, 0, 3, left))

    for zs in range(Z):
        part = slab(zs * 2 + 1 - core)
        remote(part, part, dd_send.at[zs], dd_recv.at[zs], r, c).wait_recv()
    a_wait(left, 1)
    a_wait(right, 0)
    a_wait(across, 0)
    a_wait(across, 1)

    def split_columns(step, carry):
        xq, s = step // 2, step % 2
        flat = mbuf.at[xq, s].reshape(256, 128)
        for m in range(2):
            high, low = split(flat[pl.ds(m, 128, stride=2), :])
            at = pl.ds(pl.multiple_of(s * 128, 128), 128)
            m_high[xq, at, m * 128 : (m + 1) * 128] = high
            m_low[xq, at, m * 128 : (m + 1) * 128] = low
        return carry

    lax.fori_loop(0, 8, split_columns, 0)

    def multiply(rb, carry):
        acc = jnp.zeros((128, 256), F32)
        for xq in range(4):
            both = [abuf[xq, pl.ds(rb * 256 + s, 128, stride=2), :] for s in range(2)]
            acc = acc + mm3(jnp.concatenate(both, axis=1), m_high[xq], m_low[xq])
        for m in range(2):
            pt[rb, m] = acc[:, m * 128 : (m + 1) * 128].T
        return carry

    lax.fori_loop(0, 4, multiply, 0)

    for blk in range(8):
        to_y = 2 * x + blk // X
        to_col = to_y * X + blk % X
        src = pt.at[:, :, pl.ds(blk * 16, 16)]
        here = to_col == c
        copy = remote(src, cr.at[y], rs_send.at[blk], rs_recv.at[y], r, to_col)

        @pl.when(jnp.logical_not(here))
        def _():
            copy.start()

        @pl.when(here)
        def _():
            cr[y] = pt[:, :, pl.ds(blk * 16, 16)]

    def r_wait(slot, half):
        r_move(slot, half, 0, right).wait_recv()

    r_wait(left, 0)
    start(r_move(left, 0, 4, right))
    r_wait(right, 1)
    start(r_move(right, 1, 5, left))

    from_x = y // 2
    for ys in range(8):
        here = jnp.logical_and(ys == y, from_x == x)
        copy = remote(
            pt.at[:, :, pl.ds(0, 16)], cr.at[ys], rs_send.at[0], rs_recv.at[ys],
            r, ys * X + from_x,
        )

        @pl.when(jnp.logical_not(here))
        def _():
            copy.wait_recv()

    first, second = [], []
    for a in range(4):
        sum1, sum2 = cr[0, a, 0], cr[0, a, 1]
        for ys in range(1, 8):
            sum1 = sum1 + cr[ys, a, 0]
            sum2 = sum2 + cr[ys, a, 1]
        sum1 = -keep1[a : a + 1] * sum1
        sum2 = -keep2[a : a + 1] * sum2
        cross1_ref[a] = sum1
        cross2_ref[a] = sum2
        first.append(sum1)
        second.append(sum2)
    both = jnp.concatenate(
        [jnp.concatenate(first, axis=1), jnp.concatenate(second, axis=1)], axis=0
    )
    c_high, c_low = split(both)

    r_wait(left, 1)
    r_wait(right, 0)
    r_wait(across, 0)
    r_wait(across, 1)

    rows_all = rbuf.reshape(4096, 128)
    for q in range(8):
        high, low = split(rows_all[pl.ds(q, 512, stride=8), :])
        tt[q] = mm(c_high, high) + (mm(c_low, high) + mm(c_high, low))

    q1 = jnp.concatenate([tt[k, 0:16] for k in range(4)], axis=1)
    rows = mm3(q1, s_high[...], s_low[...])
    for k in range(4):
        ls[k] = rows[:, k * 128 : (k + 1) * 128] - tt[4 + k, 0:16]
        for half in range(2):
            ts[k * 2 + half] = tt[k, half * 8 : half * 8 + 8]
            ts[8 + k * 2 + half] = tt[4 + k, 16 + half * 8 : 24 + half * 8]

    def send_link(q, carry):
        copy = remote(ls.at[q], lr.at[r], l_send.at[q], l_recv.at[r], 4 * q, c)

        @pl.when(r != 4 * q)
        def _():
            copy.start()

        return carry

    lax.fori_loop(0, 4, send_link, 0)

    def send_sum(d, carry):
        to = (r + d) % NR
        remote(ts.at[to], tr.at[r], t_send.at[d], t_recv.at[r], to, c).start()
        return carry

    lax.fori_loop(1, NR, send_sum, 0)
    tr[r] = ts[r]
    q_own = r // 4
    collects = r % 4 == 0

    @pl.when(collects)
    def _():
        lr[r] = ls[q_own]

        def take(d, carry):
            src = (r + d) % NR
            remote(ls.at[0], lr.at[src], l_send.at[0], l_recv.at[src], src, c).wait_recv()
            return carry

        lax.fori_loop(1, NR, take, 0)
        total = lr[0]
        for src in range(1, NR):
            total = total + lr[src]
        lsum[...] = total - r0[q_own]
        for j in range(8):
            to_col = 8 * q_own + j
            copy = remote(lsum, gb.at[c], g_send.at[j], g_recv.at[c], r, to_col)

            @pl.when(to_col != c)
            def _():
                copy.start()

    def take_sum(d, carry):
        src = (r + d) % NR
        remote(ts.at[0], tr.at[src], t_send.at[0], t_recv.at[src], src, c).wait_recv()
        return carry

    lax.fori_loop(1, NR, take_sum, 0)
    total = tr[0]
    for src in range(1, NR):
        total = total + tr[src]
    tsum[...] = total
    tg[r] = total

    def send_total(d, carry):
        to = (r + d) % NR
        remote(tsum, tg.at[r], tg_send.at[d], tg_recv.at[r], to, c).start()
        return carry

    lax.fori_loop(1, NR, send_total, 0)

    root_row = 4 * (c // 8)
    is_root = r == root_row

    @pl.when(is_root)
    def _():
        gb[c] = lsum[...]

        def take(d, carry):
            src = (c + d) % NC
            remote(lsum, gb.at[src], g_send.at[0], g_recv.at[src], r, src).wait_recv()
            return carry

        lax.fori_loop(1, NC, take, 0)
        for k in range(4):
            block = gb[8 * k : 8 * k + 8].reshape(128, 128)
            xt[k] = block.T
        for k in range(4):
            lk[:, k * 128 : (k + 1) * 128] = xt[k, pl.ds(pl.multiple_of(16 * (c % 8), 16), 16), :]

        def send_on(d, carry):
            to = (r + d) % NR
            remote(lk, lk, b_send.at[d], b_recv, to, c).start()
            return carry

        lax.fori_loop(1, NR, send_on, 0)

    def take_total(d, carry):
        src = (r + d) % NR
        remote(tsum, tg.at[src], tg_send.at[0], tg_recv.at[src], src, c).wait_recv()
        return carry

    lax.fori_loop(1, NR, take_total, 0)
    for k in range(4):
        lanes = slice(k * 128, (k + 1) * 128)
        sum1 = jnp.concatenate([tg[2 * k], tg[2 * k + 1]], axis=0)
        diag1_ref[:, lanes] = d1_ref[:, lanes] - sum1

    @pl.when(jnp.logical_not(is_root))
    def _():
        remote(lk, lk, b_send.at[0], b_recv, root_row, c).wait_recv()

    link = lk[...]
    link_ref[...] = link
    tail = mm3(link, s_high[...], s_low[...])
    for k in range(4):
        lanes = slice(k * 128, (k + 1) * 128)
        sum2 = jnp.concatenate([tg[8 + 2 * k], tg[9 + 2 * k]], axis=0)
        diag2_ref[:, lanes] = d2_ref[:, lanes] - (sum2 + tail[:, lanes])

    for copy in sent:
        copy.wait_send()
    for yh in range(2):
        for k in range(4):
            to_col = (r // X + 4 * yh) * X + k
            here = jnp.logical_and(c // 2 == r, c == to_col)

            @pl.when(jnp.logical_not(here))
            def _():
                remote(
                    own.at[yh, k], mbuf.at[xs, :, c], sc_send.at[yh, k], sc_recv.at[xs, c % 2],
                    c // 2, to_col,
                ).wait_send()

    for blk in range(8):
        to_col = (2 * x + blk // X) * X + blk % X

        @pl.when(to_col != c)
        def _():
            remote(
                pt.at[:, :, pl.ds(blk * 16, 16)], cr.at[y], rs_send.at[blk], rs_recv.at[y],
                r, to_col,
            ).wait_send()

    def link_left(q, carry):
        @pl.when(r != 4 * q)
        def _():
            remote(ls.at[q], lr.at[r], l_send.at[q], l_recv.at[r], 4 * q, c).wait_send()

        return carry

    lax.fori_loop(0, 4, link_left, 0)

    def sums_left(d, carry):
        to = (r + d) % NR
        remote(ts.at[to], tr.at[r], t_send.at[d], t_recv.at[r], to, c).wait_send()
        remote(tsum, tg.at[r], tg_send.at[d], tg_recv.at[r], to, c).wait_send()
        return carry

    lax.fori_loop(1, NR, sums_left, 0)

    @pl.when(collects)
    def _():
        for j in range(8):
            to_col = 8 * q_own + j

            @pl.when(to_col != c)
            def _():
                remote(lsum, gb.at[c], g_send.at[j], g_recv.at[c], r, to_col).wait_send()

    @pl.when(is_root)
    def _():
        def on_left(d, carry):
            remote(lk, lk, b_send.at[d], b_recv, (r + d) % NR, c).wait_send()
            return carry

        lax.fori_loop(1, NR, on_left, 0)


def body(
    ainv, lhat_first, lhat_second, second_on_first, dinv_first, dinv_second, anc_first, anc_second
):
    vmem = pl.BlockSpec(memory_space=pltpu.VMEM)
    hbm = pl.BlockSpec(memory_space=pl.ANY)
    dma = pltpu.SemaphoreType.DMA
    cross = jax.ShapeDtypeStruct((4, 16, 128), F32)
    panel = jax.ShapeDtypeStruct((16, 512), F32)
    cross1, diag1, cross2, link, diag2 = pl.pallas_call(
        kernel,
        out_shape=(cross, panel, cross, panel, panel),
        in_specs=[hbm, hbm] + [vmem] * 6,
        out_specs=(vmem,) * 5,
        scratch_shapes=[
            pltpu.VMEM((4, 1024, 128), F32),
            pltpu.VMEM((512, 512), F32),
            pltpu.VMEM((512, 512), BF16),
            pltpu.VMEM((512, 512), BF16),
            pltpu.VMEM((4, 8, 4, 32, 128), F32),
            pltpu.VMEM((2, 4, 2, 8, 128), F32),
            pltpu.VMEM((4, 2, 32, 8, 128), F32),
            pltpu.VMEM((4, 256, 256), BF16),
            pltpu.VMEM((4, 256, 256), BF16),
            pltpu.VMEM((4, 2, 128, 128), F32),
            pltpu.VMEM((8, 4, 2, 16, 128), F32),
            pltpu.VMEM((8, 32, 128), F32),
            pltpu.VMEM((16, 8, 128), F32),
            pltpu.VMEM((16, 8, 128), F32),
            pltpu.VMEM((4, 16, 128), F32),
            pltpu.VMEM((16, 16, 128), F32),
            pltpu.VMEM((4, 16, 128), F32),
            pltpu.VMEM((16, 8, 128), F32),
            pltpu.VMEM((8, 128), F32),
            pltpu.VMEM((32, 16, 128), F32),
            pltpu.VMEM((16, 128), F32),
            pltpu.VMEM((4, 128, 128), F32),
            pltpu.VMEM((16, 512), F32),
            dma((2,)),
            dma((6,)), dma((4, 2)),
            dma((8,)), dma((8,)),
            dma((6,)), dma((4, 2)),
            dma((2, 4)), dma((4, 2)),
            dma((8,)), dma((8,)),
            dma((8,)), dma((8,)),
            dma((8,)), dma((8,)),
            dma((16,)), dma((16,)),
            dma((4,)), dma((16,)),
            dma((16,)), dma((16,)),
            dma((8,)), dma((32,)),
            dma((16,)), dma,
        ],
        compiler_params=pltpu.CompilerParams(has_side_effects=True),
    )(
        ainv.reshape(1024, 128), second_on_first, lhat_first, lhat_second,
        dinv_first.T, dinv_second.T, anc_first.reshape(1, -1), anc_second.reshape(1, -1),
    )
    return (
        cross1.transpose(0, 2, 1), diag1.T, cross2.transpose(0, 2, 1), link.T, diag2.T,
    )


def solution(mesh):
    return jax.shard_map(
        body,
        mesh=mesh,
        in_specs=(
            P(None, "row", None, "col"),
            P(None, ("row", "col"), None),
            P(None, ("row", "col"), None),
            P(),
            P(None, "col"),
            P(None, "col"),
            P(),
            P(),
        ),
        out_specs=(
            P(None, "row", "col"),
            P(None, "col"),
            P(None, "row", "col"),
            P(None, "col"),
            P(None, "col"),
        ),
        check_vma=False,
    )
```

time: 332 us -> 117 us (0.35)
  the two profiles are of different devices: /device:TPU:1 before, /device:TPU:17 now
where the time goes in v1:
time: 117 us; the launch traced here: 116 us
  Pallas kernels  111 us (95%)
  local copies, waits for them, and re-layouts  4.31 us (4%)
    pallas_call x1, Pallas kernels, body(): pl.pallas_call(kernel, out_shape=(cross, panel, cross, panel, panel), in_...  111 us
    unnamed x13, local copies, waits for them, and re-layouts  4.31 us

profile of v1, /device:TPU:17, one launch (start us, length us, event | category | flops | bytes accessed | tf_op | source)
XLA Modules:
  0.0 116.4 jit_solution(6134371373139295076)
XLA Ops:
  0.6 111.5 %shard_map.119 = (f32[4,16,128]{2,1,0:T(8,128)}, f32[16,512]{1,0:T(8,128)}, f32[4,16,128]{2,1,0:T(8,128)}, f32[16,512]{1,0:T(8,128)}, f32[16,512]{1,0:T(8,128)}) custom-call(f32[1024,128]{1,0:T(8,128)} %bitcast.10, f32[512,512]{1,0:T(8,128)} %s_hbm.1, f32[4,4,512]{2,1,0:T(4,128)} %l1_ref.1, f32[4,4,512]{2,1,0:T(4,128)} %l2_ref.1, f32[16,512]{1,0:T(8,128)} %bitcast.11, ...), custom_call_target="tpu_custom_call" | custom-call | tf_op jit(solution)/shard_map/pallas_call | solution.py:464
  112.1 0.0 copy-start.3
  112.1 1.4 %copy.18 = f32[4,128,16]{1,2,0:T(8,128)} copy(f32[4,128,16]{1,2,0:T(8,128)} %bitcast.17) | data formatting | bytes 65536
  113.5 0.0 copy-done.3
  113.5 0.0 copy-start.2
  113.5 0.6 copy.19
  114.1 0.2 copy-done.2
  114.3 0.0 copy-start.1
  114.3 0.6 copy.20
  114.9 0.2 copy-done.1
  115.0 0.0 copy-start
  115.0 0.6 copy.21
  115.7 0.2 copy-done
  115.8 0.6 copy.22
Async XLA Ops:
  112.1 1.4 %copy-start.3 = (f32[16,512]{1,0:T(8,128)S(1)}, f32[16,512]{1,0:T(8,128)}, u32[]{:S(2)}) copy-start(f32[16,512]{1,0:T(8,128)} %get-tuple-element.11) | copy-start | bytes 98308
  113.5 0.8 copy-start.2
  114.3 0.8 copy-start.1
  115.0 0.8 copy-start
